TPU v7x, 32 devices: a whole 2x2x4 slice. The times are simulated.
32 devices in a mesh: dp: 4 (over z), mp: 8 (over y, x, core).
Axes of the slice: x: 2, y: 2, z: 4, core: 2. Of those that a mesh axis runs over, the one named last changes fastest.
Arguments:
- policy_hidden: bfloat16 [256, 3584], P('dp'), may hold values from -96 to 96
- reference_hidden: bfloat16 [256, 3584], P('dp'), may hold values from -96 to 96
- policy_gain: float32 [3584], replicated, may hold values from 0.5 to 1.5
- reference_gain: float32 [3584], replicated, may hold values from 0.5 to 1.5
- policy_embedding: bfloat16 [131072, 3584], P(('dp', 'mp')), may hold values from -1 to 1
- reference_embedding: bfloat16 [131072, 3584], P(('dp', 'mp')), may hold values from -1 to 1
- mixture_weight: float32 [256], replicated, may hold values from 0.1 to 0.9
- sampled_tokens: int32 [256], replicated, may hold values from 0 to 131071
Outputs:
- mixture_shift: float32 [256, 131072], P(None, ('dp', 'mp'))
- sampled_logprobs: float32 [3, 256], P(None, 'dp')
All inputs are finite; a program needn't handle non-finite values.
Results may differ from a plain program's by a relative error of at most 0.002.
Values may be sent and summed in bfloat16 or wider, within the bound.
A program may use at most 128 MiB of HBM per device.

v0:
```python
import jax
import jax.numpy as jnp
from jax import lax
from jax.sharding import PartitionSpec as P

softcap = 30.0
epsilon = 1e-06


def normalize(hidden, gain):
    values = hidden.astype(jnp.float32)
    meansq = jnp.mean(values * values, axis=-1, keepdims=True)
    return (values * lax.rsqrt(meansq + epsilon) * gain).astype(jnp.bfloat16)


def contract(normed, embedding):
    return lax.dot_general(
        normed, embedding, (((1,), (1,)), ((), ())), preferred_element_type=jnp.float32
    )


def local(
    policy_hidden,
    reference_hidden,
    policy_gain,
    reference_gain,
    policy_embedding,
    reference_embedding,
    mixture_weight,
    sampled_tokens,
):
    seq_local = policy_hidden.shape[0]
    vocab_local = policy_embedding.shape[0]
    stacked = jnp.stack(
        [normalize(policy_hidden, policy_gain), normalize(reference_hidden, reference_gain)]
    )
    piece = lax.all_gather(stacked, "dp", axis=1, tiled=True)
    raw = jnp.stack([contract(piece[0], policy_embedding), contract(piece[1], reference_embedding)])
    capped = softcap * jnp.tanh(raw / softcap)
    capped_policy = capped[0]
    capped_reference = capped[1]
    weight = mixture_weight[:, None]
    mixed = (1.0 - weight) * capped_policy + weight * capped_reference
    shard = lax.axis_index("dp") * lax.axis_size("mp") + lax.axis_index("mp")
    first = shard * vocab_local
    columns = lax.broadcasted_iota(jnp.int32, (1, vocab_local), 1)
    onehot = (sampled_tokens[:, None] - first == columns).astype(jnp.float32)
    terms = (
        jnp.sum(jnp.exp(capped_policy), axis=1),
        jnp.sum(jnp.exp(capped_reference), axis=1),
        jnp.sum(jnp.exp(mixed), axis=1),
        jnp.sum(onehot * capped_policy, axis=1),
        jnp.sum(onehot * capped_reference, axis=1),
    )
    policy_sum, reference_sum, mixture_sum, policy_pick, reference_pick = lax.psum(
        (terms[0], terms[1], terms[2], terms[3], terms[4]), ("dp", "mp")
    )
    policy_total = jnp.log(policy_sum)
    reference_total = jnp.log(reference_sum)
    mixture_total = jnp.log(mixture_sum)
    mixed_pick = (1.0 - mixture_weight) * policy_pick + mixture_weight * reference_pick
    policy_logp = policy_pick - policy_total
    reference_logp = reference_pick - reference_total
    mixture_logp = mixed_pick - mixture_total
    mixture_shift = mixed - mixture_total[:, None] - (capped_policy - policy_total[:, None])
    every_logp = jnp.stack([policy_logp, reference_logp, mixture_logp])
    sampled_logprobs = lax.dynamic_slice_in_dim(
        every_logp, lax.axis_index("dp") * seq_local, seq_local, 1
    )
    return (mixture_shift, sampled_logprobs)


def solution(mesh):
    in_specs = (
        P("dp", None),
        P("dp", None),
        P(),
        P(),
        P(("dp", "mp"), None),
        P(("dp", "mp"), None),
        P(),
        P(),
    )
    out_specs = (P(None, ("dp", "mp")), P(None, "dp"))
    return jax.shard_map(local, mesh=mesh, in_specs=in_specs, out_specs=out_specs, check_vma=False)
```

profile of v0, /device:TPU:0, one launch (start us, length us, event | category | flops | bytes accessed | tf_op | source)
XLA Modules:
  0.0 173.4 jit_solution(15620931690509131522)
XLA Ops:
  7.2 0.0 copy-start.1
  7.2 0.0 copy-start.2
  7.2 0.0 all-gather.2.cloned.1.call-start
  7.2 1.2 fusion.5
  8.5 1.2 fusion.2
  9.7 1.5 fusion.8
  11.2 1.0 pad_maximum_fusion
  12.2 0.0 all-gather.2.cloned.1.call-update
  12.2 0.0 copy-done.1
  12.2 0.0 copy-done.2
  12.2 74.9 %all-gather.2.cloned.1.call-done = bf16[2,256,3584]{2,1,0:T(8,128)(2,1)} async-done(((bf16[2,64,3584]{2,1,0:T(8,128)(2,1)}), bf16[2,256,3584]{2,1,0:T(8,128)(2,1)}) %all-gather.2.cloned.1.call-update) | async-done | bytes 3670032 | tf_op jit(solution)/shard_map/all_gather | solution.py:37
  87.2 14.1 %convolution_bitcast_fusion = f32[1,256,4096]{2,1,0:T(8,128)S(1)} fusion(bf16[4096,3584]{1,0:T(8,128)(2,1)} %param.13, bf16[2,256,3584]{2,1,0:T(8,128)(2,1)} %all-gather.2.cloned.1.call-done), kind=kOutput, calls=%fused_computation.3 | convolution fusion | flops 7516192768 | bytes 35389440 | tf_op jit(solution)/shard_map/dot_general | solution.py:17
  101.3 14.1 %convolution_bitcast_fusion.1 = f32[1,256,4096]{2,1,0:T(8,128)S(1)} fusion(bf16[4096,3584]{1,0:T(8,128)(2,1)} %param.12, bf16[2,256,3584]{2,1,0:T(8,128)(2,1)} %all-gather.2.cloned.1.call-done), kind=kOutput, calls=%fused_computation.4 | convolution fusion | flops 7516192768 | bytes 35389440 | tf_op jit(solution)/shard_map/dot_general | solution.py:17
  115.4 1.1 fusion.1
  116.5 0.0 copy-start
  116.6 3.5 %select_reduce_fusion = (f32[256]{0:T(256)S(1)}, f32[256]{0:T(256)S(1)}, f32[256]{0:T(256)S(1)}, f32[256]{0:T(256)S(1)}, f32[256]{0:T(256)S(1)}) fusion(f32[2,256,4096]{2,1,0:T(8,128)S(1)} %fusion.1, s32[256]{0:T(256)S(1)} %broadcast_subtract_fusion, f32[256]{0:T(256)S(1)} %copy-done.1, f32[256]{0:T(256)S(1)} %broadcast_subtract_fusion.1), kind=kLoop, calls=%fused_computation.8 | loop fusion | flops 11533056 | bytes 8396800 | tf_op jit(solution)/shard_map/reduce_sum | solution.py:53
  120.0 0.0 copy-done
  120.0 38.9 %all-reduce = (f32[256]{0:T(256)S(1)}, f32[256]{0:T(256)S(1)}, f32[256]{0:T(256)S(1)}, f32[256]{0:T(256)S(1)}, f32[256]{0:T(256)S(1)}) all-reduce(f32[256]{0:T(256)S(1)} %get-tuple-element.6, f32[256]{0:T(256)S(1)} %get-tuple-element.5, f32[256]{0:T(256)S(1)} %get-tuple-element.3, ...), channel_id=1, replica_groups=mesh['dp'=4,'mp'=8] {'dp','mp'}, use_global_device_ids=true, to_apply=%region_5.0 | all-reduce | flops 1280 | bytes 10240 | tf_op jit(solution)/shard_map/psum | solution.py:55
  158.9 7.0 %subtract_subtract_fusion = f32[256,4096]{1,0:T(8,128)} fusion(f32[2,256,4096]{2,1,0:T(8,128)} %copy-done, f32[256]{0:T(256)S(1)} %get-tuple-element.15, f32[256]{0:T(256)S(1)} %get-tuple-element.13, f32[256]{0:T(256)S(1)} %copy-done.1, f32[256]{0:T(256)S(1)} %broadcast_subtract_fusion.1), kind=kLoop, calls=%fused_computation.11 | loop fusion | flops 6291456 | bytes 12587008 | tf_op jit(solution)/shard_map/sub | solution.py:65
  165.9 0.7 fusion.11
  (5 shorter events, 0.0 us)
Async XLA Ops:
  7.2 5.0 %copy-start.1 = (f32[256]{0:T(256)S(1)}, f32[256]{0:T(256)}, u32[]{:S(2)}) copy-start(f32[256]{0:T(256)} %param.14) | copy-start | bytes 3076
  7.2 5.1 %copy-start.2 = (s32[256]{0:T(256)S(1)}, s32[256]{0:T(256)}, u32[]{:S(2)}) copy-start(s32[256]{0:T(256)} %param.15) | copy-start | bytes 3076
  7.2 80.0 %all-gather.2.cloned.1.call-start = ((), (), s32[]{:S(2)}) async-start(), calls=%async_computation | async-start | bytes 4587520 | tf_op jit(solution)/shard_map/all_gather | solution.py:37
  116.5 3.5 %copy-start = (f32[2,256,4096]{2,1,0:T(8,128)}, f32[2,256,4096]{2,1,0:T(8,128)S(1)}, u32[]{:S(2)}) copy-start(f32[2,256,4096]{2,1,0:T(8,128)S(1)} %fusion.1) | copy-start | bytes 25165828
Sparse Core Ops, SparseCore 0:
  12.3 74.8 all-gather.1
where the time goes:
time: 174 us; the launch traced here: 173 us
  waiting for transfers between devices  74.9 us (43%)
  blocking collectives  38.9 us (22%)
  matrix products  28.2 us (16%)
  other arithmetic  17.2 us (10%)
  between operations  14.1 us (8%)
    all_gather x1, waiting for transfers between devices, local(): piece = lax.all_gather(stacked, 'dp', axis=1, tiled=True)  74.9 us
    psum x1, blocking collectives, local(): lax.psum((terms[0], terms[1], terms[2], terms[3], terms[4]), ('dp', 'mp'))  38.9 us
    dot_general x2, matrix products, contract(): lax.dot_general(normed, embedding, (((1,), (1,)), ((), ())), preferred_el...  28.2 us
    sub x1, other arithmetic, local(): mixed - mixture_total[:, None] - (capped_policy - policy_total[:, None])  7.01 us
  transfers between devices with their start and end apart: 1, of which 1 were waited for; matrix products, arithmetic and copies ran while one was open for 0% of the time, Pallas kernels for 0%

commit v1 on v0

v1 whole, which is shorter than its diff:
```python
import functools

import jax
import jax.numpy as jnp
from jax import lax
from jax.experimental import pallas as pl
from jax.experimental.pallas import tpu as pltpu
from jax.sharding import PartitionSpec as P

softcap = 30.0
epsilon = 1e-06
LANES = 128
TILE = 512
SLOT_BYTES = 40 * 2**20
MESH = pl.DeviceIdType.MESH


def lane_sum(x):
    total = x[:, :LANES]
    for k in range(1, x.shape[1] // LANES):
        total = total + x[:, k * LANES : (k + 1) * LANES]
    return total


def spread(row, lanes):
    return jnp.transpose(jnp.broadcast_to(row, (LANES, row.shape[1])))[:, :lanes]


def kernel(
    n_dp,
    n_mp,
    tile,
    slots,
    ph_hbm,
    rh_hbm,
    pg_hbm,
    rg_hbm,
    pe_hbm,
    re_hbm,
    weight_ref,
    token_ref,
    diff_hbm,
    delta_ref,
    logp_ref,
    hidden,
    gains,
    normed,
    emb,
    diff,
    sums,
    weight_col,
    token_col,
    part_mp,
    part_dp,
    in_sem,
    emb_sem,
    out_sem,
    send_sem,
    recv_sem,
    fsend_sem,
    frecv_sem,
    msend_sem,
    mrecv_sem,
    dsend_sem,
    drecv_sem,
):
    dp = lax.axis_index("dp")
    mp = lax.axis_index("mp")
    half = lax.rem(mp, 2)
    partner = mp + 1 - 2 * half
    seq = hidden.shape[1]
    rows = seq // 2
    batch = normed.shape[1]
    vocab = pe_hbm.shape[0]
    tiles = vocab // tile

    loads = [
        pltpu.make_async_copy(ph_hbm, hidden.at[0], in_sem.at[0]),
        pltpu.make_async_copy(pg_hbm, gains.at[0], in_sem.at[1]),
        pltpu.make_async_copy(rh_hbm, hidden.at[1], in_sem.at[2]),
        pltpu.make_async_copy(rg_hbm, gains.at[1], in_sem.at[3]),
    ]
    for load in loads:
        load.start()

    def fetch(source, t, slot):
        return pltpu.make_async_copy(
            source.at[pl.ds(pl.multiple_of(t * tile, tile), tile)], emb.at[slot], emb_sem.at[slot]
        )

    for g in range(slots):
        fetch(pe_hbm if g < tiles else re_hbm, g % tiles, g).start()

    barrier = pltpu.get_barrier_semaphore()
    for o in range(1, n_dp):
        pl.semaphore_signal(
            barrier, inc=1, device_id={"dp": lax.rem(dp + o, n_dp)}, device_id_type=MESH
        )
    for o in range(1, n_mp):
        pl.semaphore_signal(
            barrier, inc=1, device_id={"mp": lax.rem(mp + o, n_mp)}, device_id_type=MESH
        )

    def normalize(model):
        loads[2 * model].wait()
        loads[2 * model + 1].wait()
        for r in range(0, seq, 16):
            values = hidden[model, r : r + 16].astype(jnp.float32)
            meansq = jnp.mean(values * values, axis=-1, keepdims=True)
            result = (values * lax.rsqrt(meansq + epsilon) * gains[model]).astype(jnp.bfloat16)
            normed[model, pl.ds(pl.multiple_of(dp * seq + r, 16), 16)] = result

    def my_half(model, owner):
        return normed.at[model, pl.ds(pl.multiple_of(owner * seq + half * rows, rows), rows)]

    def other_half(model, owner):
        return normed.at[
            model, pl.ds(pl.multiple_of(owner * seq + (1 - half) * rows, rows), rows)
        ]

    offsets = sorted(range(1, n_dp), key=lambda o: min(o, n_dp - o))

    def gather_copy(model, o):
        return pltpu.make_async_remote_copy(
            src_ref=my_half(model, dp),
            dst_ref=my_half(model, dp),
            send_sem=send_sem.at[model, o],
            recv_sem=recv_sem.at[model, o],
            device_id={"dp": lax.rem(dp + o, n_dp)},
            device_id_type=MESH,
        )

    def arrived(model, o):
        owner = lax.rem(dp + n_dp - o, n_dp)
        return pltpu.make_async_remote_copy(
            src_ref=my_half(model, owner),
            dst_ref=my_half(model, owner),
            send_sem=send_sem.at[model, o],
            recv_sem=recv_sem.at[model, o],
            device_id={"dp": lax.rem(dp + o, n_dp)},
            device_id_type=MESH,
        )

    def forward(model, o, part):
        owner = lax.rem(dp + n_dp - o, n_dp)
        return pltpu.make_async_remote_copy(
            src_ref=part(model, owner),
            dst_ref=part(model, owner),
            send_sem=fsend_sem.at[model, o],
            recv_sem=frecv_sem.at[model, o],
            device_id={"mp": partner},
            device_id_type=MESH,
        )

    normalize(0)
    pl.semaphore_wait(barrier, n_dp - 1 + n_mp - 1)
    for o in offsets:
        gather_copy(0, o).start()
    normalize(1)
    for o in offsets:
        gather_copy(1, o).start()

    first = (dp * n_mp + mp) * vocab
    weight = weight_ref[...]
    weight_col[...] = spread(weight, LANES)
    local_token = jnp.clip(token_ref[...] - first, -1, vocab).astype(jnp.float32)
    token_col[...] = spread(local_token, LANES)
    sums[...] = jnp.zeros_like(sums)

    def relay(model):
        for o in offsets:
            arrived(model, o).wait_recv()
            forward(model, o, my_half).start()

    def relayed(model):
        for o in offsets:
            forward(model, o, other_half).wait_recv()

    def project(model, slot):
        raw = lax.dot_general(
            normed[model],
            emb[slot],
            (((1,), (1,)), ((), ())),
            preferred_element_type=jnp.float32,
        )
        return softcap * jnp.tanh(raw * (1.0 / softcap))

    def picked(t, values):
        total = None
        lane = lax.broadcasted_iota(jnp.int32, (batch, LANES), 1)
        token = token_col[...]
        for k in range(tile // LANES):
            column = (lane + (t * tile + k * LANES)).astype(jnp.float32)
            piece = jnp.where(token == column, values[:, k * LANES : (k + 1) * LANES], 0.0)
            total = piece if total is None else total + piece
        return total

    def columns(t):
        return pl.ds(pl.multiple_of(t * tile, tile), tile)

    relay(0)
    relayed(0)

    @pl.loop(0, tiles)
    def _(t):
        slot = lax.rem(t, slots)
        fetch(pe_hbm, t, slot).wait()
        capped = project(0, slot)
        diff[:, columns(t)] = capped
        sums[0] += lane_sum(jnp.exp(capped))
        sums[3] += picked(t, capped)
        later = t + slots

        @pl.when(later < tiles)
        def _():
            fetch(pe_hbm, later, slot).start()

        @pl.when(jnp.logical_and(later >= tiles, later < 2 * tiles))
        def _():
            fetch(re_hbm, later - tiles, slot).start()

    relay(1)
    relayed(1)

    def put(t):
        return pltpu.make_async_copy(diff.at[:, columns(t)], diff_hbm.at[:, columns(t)], out_sem.at[t])

    @pl.loop(0, tiles)
    def _(t):
        g = t + tiles
        slot = lax.rem(g, slots)
        fetch(re_hbm, t, slot).wait()
        capped = project(1, slot)
        policy = diff[:, columns(t)]
        w = jnp.concatenate([weight_col[...]] * (tile // LANES), axis=1)
        mixed = (1.0 - w) * policy + w * capped
        diff[:, columns(t)] = mixed - policy
        put(t).start()
        sums[1] += lane_sum(jnp.exp(capped))
        sums[2] += lane_sum(jnp.exp(mixed))
        sums[4] += picked(t, capped)
        later = g + slots

        @pl.when(later < 2 * tiles)
        def _():
            fetch(re_hbm, later - tiles, slot).start()

    lane = lax.broadcasted_iota(jnp.int32, (batch, LANES), 1)
    packed = jnp.zeros((batch, LANES), jnp.float32)
    for k in range(5):
        packed = jnp.where(lane == k, jnp.sum(sums[k], axis=1, keepdims=True), packed)
    part_mp[0] = jnp.transpose(packed)[:8]

    def share(buffer, axis, me, n, o, send, recv):
        return pltpu.make_async_remote_copy(
            src_ref=buffer.at[0],
            dst_ref=buffer.at[o],
            send_sem=send.at[o],
            recv_sem=recv.at[o],
            device_id={axis: lax.rem(me + o, n)},
            device_id_type=MESH,
        )

    def reduce(buffer, axis, me, n, send, recv):
        for o in range(1, n):
            share(buffer, axis, me, n, o, send, recv).start()
        for o in range(1, n):
            share(buffer, axis, me, n, o, send, recv).wait_recv()
        total = buffer[0]
        for o in range(1, n):
            total = total + buffer[o]
        return total

    part_dp[0] = reduce(part_mp, "mp", mp, n_mp, msend_sem, mrecv_sem)
    total = reduce(part_dp, "dp", dp, n_dp, dsend_sem, drecv_sem)
    policy_total = jnp.log(total[0:1])
    reference_total = jnp.log(total[1:2])
    mixture_total = jnp.log(total[2:3])
    policy_pick = total[3:4]
    reference_pick = total[4:5]
    mixed_pick = (1.0 - weight) * policy_pick + weight * reference_pick
    logp_ref[0:1] = policy_pick - policy_total
    logp_ref[1:2] = reference_pick - reference_total
    logp_ref[2:3] = mixed_pick - mixture_total
    delta_ref[...] = spread(mixture_total - policy_total, LANES)

    @pl.loop(0, tiles)
    def _(t):
        put(t).wait()

    for model in range(2):
        for o in offsets:
            gather_copy(model, o).wait_send()
            forward(model, o, my_half).wait_send()
    for o in range(1, n_mp):
        share(part_mp, "mp", mp, n_mp, o, msend_sem, mrecv_sem).wait_send()
    for o in range(1, n_dp):
        share(part_dp, "dp", dp, n_dp, o, dsend_sem, drecv_sem).wait_send()


def local(
    n_dp,
    n_mp,
    policy_hidden,
    reference_hidden,
    policy_gain,
    reference_gain,
    policy_embedding,
    reference_embedding,
    mixture_weight,
    sampled_tokens,
):
    seq, width = policy_hidden.shape
    vocab = policy_embedding.shape[0]
    batch = mixture_weight.shape[0]
    tile = min(TILE, vocab)
    tiles = vocab // tile
    slots = min(2 * tiles, SLOT_BYTES // (tile * width * 2))
    anywhere = pl.BlockSpec(memory_space=pl.ANY)
    vmem = pl.BlockSpec(memory_space=pltpu.VMEM)
    dma = pltpu.SemaphoreType.DMA
    diff, delta, logp = pl.pallas_call(
        functools.partial(kernel, n_dp, n_mp, tile, slots),
        name="mixture",
        out_shape=(
            jax.ShapeDtypeStruct((batch, vocab), jnp.float32),
            jax.ShapeDtypeStruct((batch, LANES), jnp.float32),
            jax.ShapeDtypeStruct((3, batch), jnp.float32),
        ),
        in_specs=[anywhere] * 6 + [vmem] * 2,
        out_specs=(anywhere, vmem, vmem),
        scratch_shapes=[
            pltpu.VMEM((2, seq, width), jnp.bfloat16),
            pltpu.VMEM((2, 1, width), jnp.float32),
            pltpu.VMEM((2, batch, width), jnp.bfloat16),
            pltpu.VMEM((slots, tile, width), jnp.bfloat16),
            pltpu.VMEM((batch, vocab), jnp.float32),
            pltpu.VMEM((5, batch, LANES), jnp.float32),
            pltpu.VMEM((batch, LANES), jnp.float32),
            pltpu.VMEM((batch, LANES), jnp.float32),
            pltpu.VMEM((n_mp, 8, batch), jnp.float32),
            pltpu.VMEM((n_dp, 8, batch), jnp.float32),
            dma((4,)),
            dma((slots,)),
            dma((tiles,)),
            dma((2, n_dp)),
            dma((2, n_dp)),
            dma((2, n_dp)),
            dma((2, n_dp)),
            dma((n_mp,)),
            dma((n_mp,)),
            dma((n_dp,)),
            dma((n_dp,)),
        ],
        compiler_params=pltpu.CompilerParams(
            collective_id=0, has_side_effects=True, vmem_limit_bytes=57 * 2**20
        ),
    )(
        policy_hidden,
        reference_hidden,
        policy_gain.reshape(1, width),
        reference_gain.reshape(1, width),
        policy_embedding,
        reference_embedding,
        mixture_weight.reshape(1, batch),
        sampled_tokens.reshape(1, batch),
    )
    mixture_shift = diff - delta[:, :1]
    sampled_logprobs = lax.dynamic_slice_in_dim(logp, lax.axis_index("dp") * seq, seq, 1)
    return (mixture_shift, sampled_logprobs)


def solution(mesh):
    in_specs = (
        P("dp", None),
        P("dp", None),
        P(),
        P(),
        P(("dp", "mp"), None),
        P(("dp", "mp"), None),
        P(),
        P(),
    )
    out_specs = (P(None, ("dp", "mp")), P(None, "dp"))
    body = functools.partial(local, mesh.shape["dp"], mesh.shape["mp"])
    return jax.shard_map(body, mesh=mesh, in_specs=in_specs, out_specs=out_specs, check_vma=False)
```

time: 174 us -> 89.3 us (0.51)
  Pallas kernels: 0 us -> 78.5 us
  waiting for transfers between devices: 74.9 us -> 0 us
  blocking collectives: 38.9 us -> 0 us
  matrix products: 28.2 us -> 0 us
  between operations: 14.1 us -> 0.65 us
  other arithmetic: 17.2 us -> 4.79 us
  local copies, waits for them, and re-layouts: 0.01 us -> 4.97 us
    pallas_call x0 -> x1, Pallas kernels: none -> 78.5 us  [local(): pl.pallas_call(functools.partial(kernel, n_dp, n_mp, tile, slots), name='...]
    all_gather x1 -> x0, waiting for transfers between devices: 74.9 us -> none  [local(): piece = lax.all_gather(stacked, 'dp', axis=1, tiled=True)]
    psum x1 -> x0, blocking collectives: 38.9 us -> none  [local(): lax.psum((terms[0], terms[1], terms[2], terms[3], terms[4]), ('dp', 'mp'))]
    dot_general x2 -> x0, matrix products: 28.2 us -> none  [contract(): lax.dot_general(normed, embedding, (((1,), (1,)), ((), ())), preferred_el...]
    reduce_sum x3 -> x0, other arithmetic: 5.89 us -> none  [the longest x1 3.46 us: local(): jnp.sum(onehot * capped_reference, axis=1)]
    another operation x3 -> x0, other arithmetic: 3.13 us -> none  [the longest x2 2.48 us: local(): jnp.stack([normalize(policy_hidden, policy_gain), normalize(reference_hid...]
    reshape x0 -> x2, local copies, waits for them, and re-layouts: none -> 2.65 us  [the longest x1 1.33 us: local(): policy_gain.reshape(1, width)]
    sub x4 -> x1, other arithmetic: 7.02 us -> 4.79 us  [local(): mixture_shift = diff - delta[:, :1]]
  transfers between devices with their start and end apart: 1 -> 0, of which waited for: 1 -> 0; matrix products, arithmetic and copies ran while one was open for 0% -> 0% of each run, Pallas kernels for 0% -> 0%
where the time goes in v1:
time: 89.3 us; the launch traced here: 88.9 us
  Pallas kernels  78.5 us (88%)
  local copies, waits for them, and re-layouts  4.97 us (6%)
  other arithmetic  4.79 us (5%)
    pallas_call x1, Pallas kernels, local(): pl.pallas_call(functools.partial(kernel, n_dp, n_mp, tile, slots), name='...  78.5 us
    sub x1, other arithmetic, local(): mixture_shift = diff - delta[:, :1]  4.79 us

profile of v1, /device:TPU:0, one launch (start us, length us, event | category | flops | bytes accessed | tf_op | source)
XLA Modules:
  0.0 88.9 jit_solution(8513471087106102924)
XLA Ops:
  0.6 1.3 %reshape.16.pg_hbm = f32[1,3584]{1,0:T(1,128)} reshape(f32[3584]{0:T(1024)} %param.10) | data formatting | bytes 28672 | tf_op jit(solution)/shard_map/reshape | solution.py:361
  2.0 1.3 %reshape.17.rg_hbm = f32[1,3584]{1,0:T(1,128)} reshape(f32[3584]{0:T(1024)} %param.11) | data formatting | bytes 28672 | tf_op jit(solution)/shard_map/reshape | solution.py:362
  3.3 78.5 %mixture.1 = (f32[256,4096]{1,0:T(8,128)}, f32[256,128]{1,0:T(8,128)}, f32[3,256]{1,0:T(4,128)}) custom-call(bf16[64,3584]{1,0:T(8,128)(2,1)} %ph_hbm.1, bf16[64,3584]{1,0:T(8,128)(2,1)} %rh_hbm.1, f32[1,3584]{1,0:T(1,128)} %reshape.16.pg_hbm, f32[1,3584]{1,0:T(1,128)} %reshape.17.rg_hbm, bf16[4096,3584]{1,0:T(8,128)(2,1)} %pe_hbm.1, ...), custom_call_target="tpu_custom_call" | custom-call | tf_op jit(solution)/shard_map/mixture/pallas_call | solution.py:322
  81.8 1.3 %constant_dynamic-slice_fusion = f32[3,64]{1,0:T(4,128)} fusion(f32[3,256]{1,0:T(4,128)} %get-tuple-element.7, s32[]{:T(128)S(6)} %select_n.3), kind=kLoop, calls=%fused_computation.2 | loop fusion | bytes 1540 | tf_op jit(solution)/shard_map/dynamic_slice | solution.py:369
  83.1 1.0 %slice_reduce_fusion = f32[256]{0:T(256)S(1)} fusion(f32[256,128]{1,0:T(8,128)} %get-tuple-element.6), kind=kLoop, calls=%fused_computation.1 | loop fusion | bytes 2048 | tf_op jit(solution)/shard_map/slice | solution.py:368
  84.1 4.8 %broadcast_subtract_fusion = f32[256,4096]{1,0:T(8,128)} fusion(f32[256,4096]{1,0:T(8,128)} %get-tuple-element.5, f32[256]{0:T(256)S(1)} %slice_reduce_fusion), kind=kLoop, calls=%fused_computation | loop fusion | flops 1048576 | bytes 8389632 | tf_op jit(solution)/shard_map/sub | solution.py:368

commit v2 on v1

--- a/solution.py
+++ b/solution.py
@@ -59,6 +59,8 @@
     recv_sem,
     fsend_sem,
     frecv_sem,
+    psend_sem,
+    precv_sem,
     msend_sem,
     mrecv_sem,
     dsend_sem,
@@ -67,9 +69,13 @@
     dp = lax.axis_index("dp")
     mp = lax.axis_index("mp")
     half = lax.rem(mp, 2)
-    partner = mp + 1 - 2 * half
     seq = hidden.shape[1]
-    rows = seq // 2
+    group = 2 * (seq // 16)
+    width = hidden.shape[2] // 2
+    me = lax.rem(mp, group)
+    base = mp - me
+    twin = me + 1 - 2 * half
+    hops = range(2, group, 2)
     batch = normed.shape[1]
     vocab = pe_hbm.shape[0]
     tiles = vocab // tile
@@ -110,20 +116,17 @@
             result = (values * lax.rsqrt(meansq + epsilon) * gains[model]).astype(jnp.bfloat16)
             normed[model, pl.ds(pl.multiple_of(dp * seq + r, 16), 16)] = result
 
-    def my_half(model, owner):
-        return normed.at[model, pl.ds(pl.multiple_of(owner * seq + half * rows, rows), rows)]
-
-    def other_half(model, owner):
-        return normed.at[
-            model, pl.ds(pl.multiple_of(owner * seq + (1 - half) * rows, rows), rows)
-        ]
+    def block(model, owner, member):
+        row = pl.multiple_of(owner * seq + member // 2 * 16, 16)
+        column = pl.multiple_of(lax.rem(member, 2) * width, 128)
+        return normed.at[model, pl.ds(row, 16), pl.ds(column, width)]
 
     offsets = sorted(range(1, n_dp), key=lambda o: min(o, n_dp - o))
 
     def gather_copy(model, o):
         return pltpu.make_async_remote_copy(
-            src_ref=my_half(model, dp),
-            dst_ref=my_half(model, dp),
+            src_ref=block(model, dp, me),
+            dst_ref=block(model, dp, me),
             send_sem=send_sem.at[model, o],
             recv_sem=recv_sem.at[model, o],
             device_id={"dp": lax.rem(dp + o, n_dp)},
@@ -133,22 +136,36 @@
     def arrived(model, o):
         owner = lax.rem(dp + n_dp - o, n_dp)
         return pltpu.make_async_remote_copy(
-            src_ref=my_half(model, owner),
-            dst_ref=my_half(model, owner),
+            src_ref=block(model, owner, me),
+            dst_ref=block(model, owner, me),
             send_sem=send_sem.at[model, o],
             recv_sem=recv_sem.at[model, o],
             device_id={"dp": lax.rem(dp + o, n_dp)},
             device_id_type=MESH,
         )
 
-    def forward(model, o, part):
+    def member_of(index, q):
+        return lax.rem(index + group - q, group)
+
+    def pass_on(model, o, q, member):
         owner = lax.rem(dp + n_dp - o, n_dp)
         return pltpu.make_async_remote_copy(
-            src_ref=part(model, owner),
-            dst_ref=part(model, owner),
-            send_sem=fsend_sem.at[model, o],
-            recv_sem=frecv_sem.at[model, o],
-            device_id={"mp": partner},
+            src_ref=block(model, owner, member),
+            dst_ref=block(model, owner, member),
+            send_sem=psend_sem.at[model, o, q],
+            recv_sem=precv_sem.at[model, o, q],
+            device_id={"mp": base + lax.rem(me + q, group)},
+            device_id_type=MESH,
+        )
+
+    def forward(model, o, q, member):
+        owner = lax.rem(dp + n_dp - o, n_dp)
+        return pltpu.make_async_remote_copy(
+            src_ref=block(model, owner, member),
+            dst_ref=block(model, owner, member),
+            send_sem=fsend_sem.at[model, o, q],
+            recv_sem=frecv_sem.at[model, o, q],
+            device_id={"mp": base + twin},
             device_id_type=MESH,
         )
 
@@ -170,11 +187,19 @@
     def relay(model):
         for o in offsets:
             arrived(model, o).wait_recv()
-            forward(model, o, my_half).start()
+            for q in hops:
+                pass_on(model, o, q, me).start()
+            forward(model, o, 0, me).start()
+        for o in offsets:
+            for q in hops:
+                member = member_of(me, q)
+                pass_on(model, o, q, member).wait_recv()
+                forward(model, o, q, member).start()
 
     def relayed(model):
         for o in offsets:
-            forward(model, o, other_half).wait_recv()
+            for q in range(0, group, 2):
+                forward(model, o, q, member_of(twin, q)).wait_recv()
 
     def project(model, slot):
         raw = lax.dot_general(
@@ -279,9 +304,12 @@
     policy_pick = total[3:4]
     reference_pick = total[4:5]
     mixed_pick = (1.0 - weight) * policy_pick + weight * reference_pick
-    logp_ref[0:1] = policy_pick - policy_total
-    logp_ref[1:2] = reference_pick - reference_total
-    logp_ref[2:3] = mixed_pick - mixture_total
+    logp = (policy_pick - policy_total, reference_pick - reference_total, mixed_pick - mixture_total)
+    for k, row in enumerate(logp):
+        mine = row[:, :seq]
+        for owner in range(1, n_dp):
+            mine = jnp.where(dp == owner, row[:, owner * seq : (owner + 1) * seq], mine)
+        logp_ref[k : k + 1] = mine
     delta_ref[...] = spread(mixture_total - policy_total, LANES)
 
     @pl.loop(0, tiles)
@@ -291,7 +319,10 @@
     for model in range(2):
         for o in offsets:
             gather_copy(model, o).wait_send()
-            forward(model, o, my_half).wait_send()
+            for q in hops:
+                pass_on(model, o, q, me).wait_send()
+            for q in range(0, group, 2):
+                forward(model, o, q, member_of(me, q)).wait_send()
     for o in range(1, n_mp):
         share(part_mp, "mp", mp, n_mp, o, msend_sem, mrecv_sem).wait_send()
     for o in range(1, n_dp):
@@ -316,6 +347,7 @@
     tile = min(TILE, vocab)
     tiles = vocab // tile
     slots = min(2 * tiles, SLOT_BYTES // (tile * width * 2))
+    group = 2 * (seq // 16)
     anywhere = pl.BlockSpec(memory_space=pl.ANY)
     vmem = pl.BlockSpec(memory_space=pltpu.VMEM)
     dma = pltpu.SemaphoreType.DMA
@@ -325,7 +357,7 @@
         out_shape=(
             jax.ShapeDtypeStruct((batch, vocab), jnp.float32),
             jax.ShapeDtypeStruct((batch, LANES), jnp.float32),
-            jax.ShapeDtypeStruct((3, batch), jnp.float32),
+            jax.ShapeDtypeStruct((3, seq), jnp.float32),
         ),
         in_specs=[anywhere] * 6 + [vmem] * 2,
         out_specs=(anywhere, vmem, vmem),
@@ -345,8 +377,10 @@
             dma((tiles,)),
             dma((2, n_dp)),
             dma((2, n_dp)),
-            dma((2, n_dp)),
-            dma((2, n_dp)),
+            dma((2, n_dp, group)),
+            dma((2, n_dp, group)),
+            dma((2, n_dp, group)),
+            dma((2, n_dp, group)),
             dma((n_mp,)),
             dma((n_mp,)),
             dma((n_dp,)),
@@ -366,8 +400,7 @@
         sampled_tokens.reshape(1, batch),
     )
     mixture_shift = diff - delta[:, :1]
-    sampled_logprobs = lax.dynamic_slice_in_dim(logp, lax.axis_index("dp") * seq, seq, 1)
-    return (mixture_shift, sampled_logprobs)
+    return (mixture_shift, logp)
 
 
 def solution(mesh):

time: 89.3 us -> 80 us (0.90)
  Pallas kernels: 78.5 us -> 69.9 us
    pallas_call x1, Pallas kernels: 78.5 us -> 69.9 us  [local(): pl.pallas_call(functools.partial(kernel, n_dp, n_mp, tile, slots), name='...]
    dynamic_slice x1 -> x0, local copies, waits for them, and re-layouts: 1.31 us -> none  [local(): lax.dynamic_slice_in_dim(logp, lax.axis_index('dp') * seq, seq, 1)]
where the time goes in v2:
time: 80 us; the launch traced here: 79.6 us
  Pallas kernels  69.9 us (87%)
  other arithmetic  4.79 us (6%)
  local copies, waits for them, and re-layouts  4.24 us (5%)
    pallas_call x1, Pallas kernels, local(): pl.pallas_call(functools.partial(kernel, n_dp, n_mp, tile, slots), name='...  69.9 us
    sub x1, other arithmetic, local(): mixture_shift = diff - delta[:, :1]  4.79 us

profile of v2, /device:TPU:0, one launch (start us, length us, event | category | flops | bytes accessed | tf_op | source)
XLA Modules:
  0.0 79.6 jit_solution(13979478070994967393)
XLA Ops:
  0.6 1.3 %reshape.16.pg_hbm = f32[1,3584]{1,0:T(1,128)} reshape(f32[3584]{0:T(1024)} %param.10) | data formatting | bytes 28672 | tf_op jit(solution)/shard_map/reshape | solution.py:395
  2.0 1.3 %reshape.17.rg_hbm = f32[1,3584]{1,0:T(1,128)} reshape(f32[3584]{0:T(1024)} %param.11) | data formatting | bytes 28672 | tf_op jit(solution)/shard_map/reshape | solution.py:396
  3.3 69.9 %mixture.1 = (f32[256,4096]{1,0:T(8,128)}, f32[256,128]{1,0:T(8,128)}, f32[3,64]{1,0:T(4,128)}) custom-call(bf16[64,3584]{1,0:T(8,128)(2,1)} %ph_hbm.1, bf16[64,3584]{1,0:T(8,128)(2,1)} %rh_hbm.1, f32[1,3584]{1,0:T(1,128)} %reshape.16.pg_hbm, f32[1,3584]{1,0:T(1,128)} %reshape.17.rg_hbm, bf16[4096,3584]{1,0:T(8,128)(2,1)} %pe_hbm.1, ...), custom_call_target="tpu_custom_call" | custom-call | tf_op jit(solution)/shard_map/mixture/pallas_call | solution.py:354
  73.2 1.0 %slice_reduce_fusion = f32[256]{0:T(256)S(1)} fusion(f32[256,128]{1,0:T(8,128)} %get-tuple-element.6), kind=kLoop, calls=%fused_computation.1 | loop fusion | bytes 2048 | tf_op jit(solution)/shard_map/slice | solution.py:402
  74.2 0.0 copy-start
  74.2 4.8 %broadcast_subtract_fusion = f32[256,4096]{1,0:T(8,128)} fusion(f32[256,4096]{1,0:T(8,128)} %get-tuple-element.5, f32[256]{0:T(256)S(1)} %slice_reduce_fusion), kind=kLoop, calls=%fused_computation | loop fusion | flops 1048576 | bytes 8389632 | tf_op jit(solution)/shard_map/sub | solution.py:402
  79.0 0.0 copy-done
  79.0 0.6 copy.11
Async XLA Ops:
  74.2 4.8 %copy-start = (f32[3,64]{1,0:T(4,128)S(1)}, f32[3,64]{1,0:T(4,128)}, u32[]{:S(2)}) copy-start(f32[3,64]{1,0:T(4,128)} %get-tuple-element.11) | copy-start | bytes 2308
